TPU v7x, 256 devices: a whole 4x4x8 slice. The times are simulated.
256 devices in a mesh: fsdp: 16 (over z, core), tp: 16 (over y, x).
Axes of the slice: x: 4, y: 4, z: 8, core: 2. Of those that a mesh axis runs over, the one named last changes fastest.
Arguments:
- w_gate: bfloat16 [4096, 11008], P('fsdp', 'tp'), may hold values from -0.09375 to 0.09375
- low_gate: bfloat16 [4096, 16], P('fsdp'), may hold values from -0.09375 to 0.09375
- high_gate: bfloat16 [16, 11008], P(None, 'tp'), may hold values from -1.5 to 1.5
- w_up: bfloat16 [4096, 11008], P('fsdp', 'tp'), may hold values from -0.09375 to 0.09375
- low_up: bfloat16 [4096, 16], P('fsdp'), may hold values from -0.09375 to 0.09375
- high_up: bfloat16 [16, 11008], P(None, 'tp'), may hold values from -1.5 to 1.5
- w_down: bfloat16 [11008, 4096], P('tp', 'fsdp'), may hold values from -0.0546875 to 0.0546875
- low_down: bfloat16 [11008, 16], P('tp'), may hold values from -0.0546875 to 0.0546875
- high_down: bfloat16 [16, 4096], P(None, 'fsdp'), may hold values from -1.5 to 1.5
- norm_train: float32 [4096], P(('fsdp', 'tp')), may hold values from 0.25 to 1.75
- norm_step: float32 [4096], P(('fsdp', 'tp')), may hold values from -0.3 to 0.3
Outputs:
- serving_gate: bfloat16 [4096, 11008], P(None, 'tp')
- serving_up: bfloat16 [4096, 11008], P(None, 'tp')
- serving_down: bfloat16 [11008, 4096], P('tp')
- serve_norm: bfloat16 [4096], replicated
All inputs are finite; a program needn't handle non-finite values.
Results may differ from a plain program's by a relative error of at most 0.001.
Values may be sent and summed in bfloat16 or wider, within the bound.
A program may use at most 128 MiB of HBM per device.

v0:
```python
import jax
import jax.numpy as jnp
from jax import lax
from jax.sharding import Mesh
from jax.sharding import PartitionSpec as P

FSDP = ("fsdp_0", "fsdp_1")
FSDP_TP = ("fsdp_0", "fsdp_1", "tp_0", "tp_1")
TP = ("tp_0", "tp_1")


mix_rate = 2.0


def gather_turned(arrays, axis, dims):
    turned = [jnp.moveaxis(a, dim, 0) for a, dim in zip(arrays, dims)]
    widths = [t[0].size for t in turned]
    both = jnp.concatenate([t.reshape(-1, w) for t, w in zip(turned, widths)], axis=1)
    whole = lax.all_gather(both, axis, axis=0, tiled=True)
    parts = jnp.split(whole, [sum(widths[:k]) for k in range(1, len(widths))], axis=1)
    return tuple(
        (
            jnp.moveaxis(b.reshape(-1, *t.shape[1:]), 0, dim)
            for b, t, dim in zip(parts, turned, dims)
        )
    )


def laid_out(parts, dim):
    parts = jnp.moveaxis(parts, 0, dim)
    dims = parts.shape
    return parts.reshape(*dims[:dim], dims[dim] * dims[dim + 1], *dims[dim + 2 :])


def all_blocks(x, axes, sequence):
    parts = x[None]
    for k in sequence:
        parts = lax.all_gather(parts, axes[k], axis=0, tiled=True)
    held = [lax.axis_size(axes[k]) for k in reversed(sequence)]
    parts = parts.reshape(*held, *x.shape)
    turned = sorted(range(len(sequence)), key=lambda place: sequence[len(sequence) - 1 - place])
    return parts.transpose(*turned, *range(len(sequence), parts.ndim)).reshape(-1, *x.shape)


def gathered_by_axis(x, axes, sequence, dim):
    return laid_out(all_blocks(x, axes, sequence), dim)


def local(
    w_gate,
    low_gate,
    high_gate,
    w_up,
    low_up,
    high_up,
    w_down,
    low_down,
    high_down,
    norm_train,
    norm_step,
):
    whole_gate = w_gate.astype(jnp.float32) + mix_rate * jnp.dot(
        low_gate, high_gate, preferred_element_type=jnp.float32
    )
    whole_up = w_up.astype(jnp.float32) + mix_rate * jnp.dot(
        low_up, high_up, preferred_element_type=jnp.float32
    )
    whole_down = w_down.astype(jnp.float32) + mix_rate * jnp.dot(
        low_down, high_down, preferred_element_type=jnp.float32
    )
    narrow_gate, narrow_up, narrow_down = (
        whole_gate.astype(jnp.bfloat16),
        whole_up.astype(jnp.bfloat16),
        whole_down.astype(jnp.bfloat16),
    )
    serving_gate, serving_up, serving_down = gather_turned(
        (narrow_gate, narrow_up, narrow_down), FSDP, (0, 0, 1)
    )
    serve_norm = gathered_by_axis(
        (norm_train + norm_step).astype(jnp.bfloat16), FSDP_TP, (0, 2, 3, 1), 0
    )
    return (serving_gate, serving_up, serving_down, serve_norm)


def solution(mesh):
    finer = Mesh(mesh.devices.reshape(8, 2, 4, 4), ("fsdp_0", "fsdp_1", "tp_0", "tp_1"))
    in_specs = (
        P(FSDP, TP),
        P(FSDP, None),
        P(None, TP),
        P(FSDP, TP),
        P(FSDP, None),
        P(None, TP),
        P(TP, FSDP),
        P(TP, None),
        P(None, FSDP),
        P(FSDP_TP),
        P(FSDP_TP),
    )
    out_specs = (P(None, TP), P(None, TP), P(TP, None), P())
    return jax.shard_map(local, mesh=finer, in_specs=in_specs, out_specs=out_specs, check_vma=False)
```

profile of v0, /device:TPU:1, one launch (start us, length us, event | category | flops | bytes accessed | tf_op | source)
XLA Modules:
  0.0 139.7 jit_solution(4759233117201555211)
XLA Ops:
  7.2 0.0 copy-start
  7.2 0.0 all-gather.4.cloned.1.call-start
  7.2 0.7 copy-done
  7.9 1.3 fusion.3
  9.2 1.3 fusion.4
  10.5 0.0 copy-start.3
  10.6 0.0 copy-start.1
  10.6 0.0 copy-start.2
  10.6 1.3 fusion.6
  11.9 1.0 pad_maximum_fusion
  12.9 0.0 all-gather.4.cloned.1.call-update
  13.0 0.0 copy-done.3
  13.0 0.6 dynamic-slice
  14.2 0.0 copy-done.1
  14.2 0.0 copy-done.2
  14.3 0.2 dynamic-update-slice
  14.5 17.3 %all-reduce = bf16[128]{0:T(256)(128)(2,1)S(1)} all-reduce(bf16[128]{0:T(256)(128)(2,1)S(1)} %dynamic-update-slice), channel_id=2, replica_groups=mesh['fsdp_0'=8,'fsdp_1'=2,'tp_0'=4,'tp_1'=4] {'fsdp_0'}, use_global_device_ids=true, to_apply=%add | all-reduce | flops 128 | bytes 512
  31.8 0.1 reshape.12
  31.9 9.7 %all_gather.17 = bf16[32,16]{1,0:T(8,128)(2,1)S(1)} all-gather(bf16[8,16]{1,0:T(8,128)(2,1)S(1)} %reshape.12), channel_id=1, replica_groups=mesh['fsdp_0'=8,'fsdp_1'=2,'tp_0'=4,'tp_1'=4] {'tp_0'}, dimensions={0}, use_global_device_ids=true | all-gather | bytes 1280 | tf_op jit(solution)/shard_map/all_gather | solution.py:38
  41.6 0.1 copy.16
  41.6 10.1 %all-gather.1 = bf16[4,32,16]{1,2,0:T(8,128)(2,1)S(1)} all-gather(bf16[1,32,16]{1,2,0:T(8,128)(2,1)S(1)} %copy.16), channel_id=1, replica_groups=mesh['fsdp_0'=8,'fsdp_1'=2,'tp_0'=4,'tp_1'=4] {'tp_1'}, dimensions={0}, use_global_device_ids=true | all-gather | bytes 5120 | tf_op jit(solution)/shard_map/all_gather | solution.py:38
  51.8 0.1 copy.17
  51.9 10.0 %all_gather.19 = bf16[256,16]{1,0:T(8,128)(2,1)S(1)} all-gather(bf16[128,16]{1,0:T(8,128)(2,1)S(1)} %bitcast.17), channel_id=1, replica_groups=mesh['fsdp_0'=8,'fsdp_1'=2,'tp_0'=4,'tp_1'=4] {'fsdp_1'}, dimensions={0}, use_global_device_ids=true | all-gather | bytes 12288 | tf_op jit(solution)/shard_map/all_gather | solution.py:38
  61.9 0.7 reshape_reshape.3
  62.6 57.0 %all-gather.4.cloned.1.call-done = bf16[4096,2064]{0,1:T(8,128)(2,1)} async-done(((bf16[256,2064]{0,1:T(8,128)(2,1)}), bf16[4096,2064]{0,1:T(8,128)(2,1)}) %all-gather.4.cloned.1.call-update) | async-done | bytes 16908304 | tf_op jit(solution)/shard_map/all_gather | solution.py:19
  119.6 13.3 %slice_bitcast_fusion = (bf16[688,4096]{1,0:T(8,128)(2,1)}, bf16[4096,688]{0,1:T(8,128)(2,1)}, bf16[4096,688]{0,1:T(8,128)(2,1)}) fusion(bf16[4096,2064]{0,1:T(8,128)(2,1)} %all-gather.4.cloned.1.call-done), kind=kLoop, calls=%fused_computation | loop fusion | bytes 33816576 | tf_op jit(solution)/shard_map/transpose | solution.py:23
  (3 shorter events, 0.0 us)
Async XLA Ops:
  7.2 0.7 copy-start
  7.2 112.4 %all-gather.4.cloned.1.call-start = ((), (), s32[]{:S(2)}) async-start(), calls=%async_computation | async-start | bytes 17965056 | tf_op jit(solution)/shard_map/all_gather | solution.py:19
  10.5 2.4 %copy-start.3 = (u32[256]{0:T(256)S(1)}, u32[256]{0:T(256)}, u32[]{:S(2)}) copy-start(u32[256]{0:T(256)} %constant.7) | copy-start | bytes 3076
  10.6 3.7 %copy-start.1 = (f32[16]{0:T(128)S(1)}, f32[16]{0:T(128)}, u32[]{:S(2)}) copy-start(f32[16]{0:T(128)} %param.20) | copy-start | bytes 196
  10.6 3.7 %copy-start.2 = (f32[16]{0:T(128)S(1)}, f32[16]{0:T(128)}, u32[]{:S(2)}) copy-start(f32[16]{0:T(128)} %param.21) | copy-start | bytes 196
Sparse Core Ops, SparseCore 0:
  13.1 106.4 all-gather.3
where the time goes:
time: 140 us
  waiting for transfers between devices  57 us (41%)
  blocking collectives  47.1 us (34%)
  local copies, waits for them, and re-layouts  15.8 us (11%)
  between operations  14.8 us (11%)
  matrix products  3.94 us (3%)
    all_gather x1, waiting for transfers between devices, gather_turned(): whole = lax.all_gather(both, axis, axis=0, tiled=True)  57 us
    all_gather x3, blocking collectives, all_blocks(): parts = lax.all_gather(parts, axes[k], axis=0, tiled=True)  29.8 us
    unnamed x1, blocking collectives  17.3 us
    transpose x1, local copies, waits for them, and re-layouts, gather_turned(): jnp.moveaxis(b.reshape(-1, *t.shape[1:]), 0, dim)  13.3 us
  transfers between devices with their start and end apart: 1, of which 1 were waited for; matrix products, arithmetic and copies ran while one was open for 1% of the time, Pallas kernels for 0%

commit v1 on v0

v1 whole, which is shorter than its diff:
```python
import functools

import jax
import jax.numpy as jnp
from jax import lax
from jax.experimental import pallas as pl
from jax.experimental.pallas import tpu as pltpu
from jax.sharding import Mesh
from jax.sharding import PartitionSpec as P

mix_rate = 2.0
MESH = pl.DeviceIdType.MESH
AXES = ("z", "core", "y", "x")
FSDP = ("z", "core")
TP = ("y", "x")
NZ, NX, NY = 8, 4, 4
ROWS = ((0, 384), (384, 304))
TILE = 128


def body(rows_total, width, *refs):
    (wg, wu, wd, ag, au, ad, bg, bu, bd, ntrain, nstep, og, ou, od, onorm,
     w_v, a_v, b_v, own, nt_v, ns_v, nz, nsib, nx, ny, nrow,
     in_sem, own_sem, r_recv, l_recv, s_recv, own_send, r_send, l_send, s_send,
     nrr, nlr, nrs, nls, nsr, nss, nxr, nxs, nyr, nys) = refs
    w_hbm, a_hbm, b_hbm, outs = (wg, wu, wd), (ag, au, ad), (bg, bu, bd), (og, ou, od)
    z, core, y, x = (lax.axis_index(k) for k in AXES)
    right, left = {"z": lax.rem(z + 1, NZ)}, {"z": lax.rem(z + NZ - 1, NZ)}
    sib = {"core": 1 - core}
    x_up, x_down = {"x": lax.rem(x + 1, NX)}, {"x": lax.rem(x + NX - 1, NX)}
    y_up, y_down = {"y": lax.rem(y + 1, NY)}, {"y": lax.rem(y + NY - 1, NY)}
    chunks = [(m, r0, n) for m in range(3) for r0, n in ROWS]
    count = len(chunks)

    loads = []
    for m in range(3):
        loads.append([
            pltpu.make_async_copy(w_hbm[m], w_v.at[m], in_sem.at[m, 0]),
            pltpu.make_async_copy(a_hbm[m], a_v.at[m], in_sem.at[m, 1]),
            pltpu.make_async_copy(b_hbm[m], b_v.at[m], in_sem.at[m, 2]),
        ])
    norm_loads = [
        pltpu.make_async_copy(ntrain, nt_v, in_sem.at[3, 0]),
        pltpu.make_async_copy(nstep, ns_v, in_sem.at[3, 1]),
    ]
    for m in range(3):
        for copy in loads[m]:
            copy.start()
    for copy in norm_loads:
        copy.start()

    barrier = pltpu.get_barrier_semaphore()
    for device in (right, left, sib, x_up, x_down, y_up, y_down):
        pl.semaphore_signal(barrier, inc=1, device_id=device, device_id_type=MESH)

    def columns(block_z, block_core):
        at = (block_z * 2 + block_core) * width
        return pl.ds(pl.multiple_of(at, width), width)

    def spot(k, block_z, block_core):
        m, r0, n = chunks[k]
        return outs[m].at[pl.ds(r0, n), columns(block_z, block_core)]

    def mine(k):
        m, r0, n = chunks[k]
        return own.at[m, pl.ds(r0, n), :]

    def remote(src, dst, send, recv, device):
        return pltpu.make_async_remote_copy(
            src_ref=src, dst_ref=dst, send_sem=send, recv_sem=recv, device_id=device, device_id_type=MESH)

    half = count // 2

    def r_copy(step, k):
        block = lax.rem(z + NZ - step, NZ)
        src = mine(k) if step == 0 else spot(k, block, core)
        return remote(src, spot(k, block, core), r_send.at[step, k], r_recv.at[step, k], right)

    def l_copy(step, k):
        block = lax.rem(z + step, NZ)
        src = mine(k) if step == 0 else spot(k, block, core)
        return remote(src, spot(k, block, core), l_send.at[step, k], l_recv.at[step, k], left)

    def arrived(sem, step, k, block):
        return remote(spot(k, block, core), spot(k, block, core), r_send.at[0, 0], sem.at[step, k], right)

    def s_copy(dist, k):
        block = lax.rem(z + dist, NZ)
        src = mine(k) if dist == 0 else spot(k, block, core)
        return remote(src, spot(k, block, core), s_send.at[dist, k], s_recv.at[dist, k], sib)

    def s_arrived(dist, k):
        block = lax.rem(z + dist, NZ)
        return remote(spot(k, block, 1 - core), spot(k, block, 1 - core), s_send.at[dist, k], s_recv.at[dist, k], sib)

    def compute(k):
        m, r0, n = chunks[k]
        for at in range(r0, r0 + n, TILE):
            size = min(TILE, r0 + n - at)
            delta = lax.dot_general(
                a_v[m, :, at:at + size], b_v[m], (((0,), (0,)), ((), ())), preferred_element_type=jnp.float32)
            whole = w_v[m, at:at + size, :].astype(jnp.float32) + mix_rate * delta
            own[m, at:at + size, :] = whole.astype(jnp.bfloat16)

    started = []

    def go(copy):
        copy.start()
        started.append(copy)

    own_copies = []

    def send_own(k):
        go(r_copy(0, k))
        go(l_copy(0, k))
        go(s_copy(0, k))
        copy = pltpu.make_async_copy(mine(k), spot(k, z, core), own_sem.at[k])
        copy.start()
        own_copies.append(copy)

    for k in range(count):
        m = chunks[k][0]
        if k == 0 or chunks[k - 1][0] != m:
            for copy in loads[m]:
                copy.wait()
        compute(k)
        if k == 1:
            pl.semaphore_wait(barrier, 7)
        if k >= 1:
            send_own(k - 1)

    for copy in norm_loads:
        copy.wait()
    gain = (nt_v[...] + ns_v[...]).astype(jnp.bfloat16)
    t = y * NX + x
    lane = lax.broadcasted_iota(jnp.int32, (16, 128), 1)
    entry = lax.broadcasted_iota(jnp.int32, (16, 128), 0)
    place = jnp.where(lane == lax.rem(t, 8) * 16 + entry, 1.0, 0.0).astype(jnp.bfloat16)
    spread = jnp.dot(jnp.broadcast_to(gain, (16, 16)), place, preferred_element_type=jnp.float32)[:8]
    row = lax.broadcasted_iota(jnp.int32, (8, 128), 0)
    nz[z] = jnp.where(row == core * 2 + t // 8, spread, 0.0)
    send_own(count - 1)

    def norm_r(step):
        block = lax.rem(z + NZ - step, NZ)
        return remote(nz.at[block], nz.at[block], nrs.at[step], nrr.at[step], right)

    def norm_r_arrived(step):
        block = lax.rem(z + NZ - step - 1, NZ)
        return remote(nz.at[block], nz.at[block], nrs.at[step], nrr.at[step], right)

    def norm_l(step):
        block = lax.rem(z + step, NZ)
        return remote(nz.at[block], nz.at[block], nls.at[step], nlr.at[step], left)

    def norm_l_arrived(step):
        block = lax.rem(z + step + 1, NZ)
        return remote(nz.at[block], nz.at[block], nls.at[step], nlr.at[step], left)

    def norm_start():
        go(norm_r(0))
        go(norm_l(0))

    def norm_step(step):
        def act():
            norm_r_arrived(step).wait_recv()
            if step < 3:
                go(norm_r(step + 1))
                norm_l_arrived(step).wait_recv()
                if step < 2:
                    go(norm_l(step + 1))
        return act

    sib_norm = remote(nz, nsib, nss, nsr, sib)

    def x_copy(step):
        return remote(nx.at[step], nx.at[step + 1], nxs.at[step], nxr.at[step], x_up)

    def y_copy(step):
        return remote(ny.at[step], ny.at[step + 1], nys.at[step], nyr.at[step], y_up)

    def norm_sib():
        go(sib_norm)

    def norm_x0():
        sib_norm.wait_recv()
        nx[0] = nz[...] + nsib[...]

    def norm_x(step):
        def act():
            if step > 0:
                x_copy(step - 1).wait_recv()
            if step < 3:
                go(x_copy(step))
            else:
                ny[0] = nx[0] + nx[1] + nx[2] + nx[3]
        return act

    def norm_y(step):
        def act():
            if step > 0:
                y_copy(step - 1).wait_recv()
            if step < 3:
                go(y_copy(step))
            else:
                whole = ny[0] + ny[1] + ny[2] + ny[3]
                for k in range(NZ):
                    nrow[4 * k:4 * k + 4, :] = whole[k, 0:4, :]
                onorm[...] = nrow[...].astype(jnp.bfloat16)
        return act

    acts = [norm_start] + [norm_step(k) for k in range(4)] + [norm_sib, norm_x0]
    acts += [norm_x(k) for k in range(4)] + [norm_y(k) for k in range(4)]

    for step in range(4):
        for k in range(count):
            if step < 3 or k < half:
                block = lax.rem(z + NZ - step - 1, NZ)
                arrived(r_recv, step, k, block).wait_recv()
                if step < 2 or (step == 2 and k < half):
                    go(r_copy(step + 1, k))
                go(s_copy(NZ - step - 1, k))
            if step < 3 or k >= half:
                block = lax.rem(z + step + 1, NZ)
                arrived(l_recv, step, k, block).wait_recv()
                if step < 2 or (step == 2 and k >= half):
                    go(l_copy(step + 1, k))
                go(s_copy(step + 1, k))
            if acts:
                acts.pop(0)()
    while acts:
        acts.pop(0)()

    for copy in own_copies:
        copy.wait()
    for copy in started:
        copy.wait_send()
    for dist in range(NZ):
        for k in range(count):
            s_arrived(dist, k).wait_recv()


def gathered(*args):
    w, a, b, norms = args[0:3], args[3:6], args[6:9], args[9:11]
    rows, width = w[0].shape
    rank = a[0].shape[0]
    count = 3 * len(ROWS)
    whole = jax.ShapeDtypeStruct((rows, width * 16), jnp.bfloat16)
    anywhere = pl.BlockSpec(memory_space=pl.ANY)
    dma = pltpu.SemaphoreType.DMA
    f32 = jnp.float32
    return pl.pallas_call(
        functools.partial(body, rows, width),
        out_shape=(whole, whole, whole, jax.ShapeDtypeStruct((32, 128), jnp.bfloat16)),
        in_specs=[anywhere] * 11,
        out_specs=(anywhere, anywhere, anywhere, pl.BlockSpec(memory_space=pltpu.VMEM)),
        scratch_shapes=[
            pltpu.VMEM((3, rows, width), jnp.bfloat16),
            pltpu.VMEM((3, rank, rows), jnp.bfloat16),
            pltpu.VMEM((3, rank, width), jnp.bfloat16),
            pltpu.VMEM((3, rows, width), jnp.bfloat16),
            pltpu.VMEM((1, 16), f32),
            pltpu.VMEM((1, 16), f32),
            pltpu.VMEM((8, 8, 128), f32),
            pltpu.VMEM((8, 8, 128), f32),
            pltpu.VMEM((4, 8, 8, 128), f32),
            pltpu.VMEM((4, 8, 8, 128), f32),
            pltpu.VMEM((32, 128), f32),
            dma((4, 3)), dma((count,)),
            dma((4, count)), dma((4, count)), dma((8, count)),
            dma((1,)), dma((4, count)), dma((4, count)), dma((8, count)),
            dma((4,)), dma((4,)), dma((4,)), dma((4,)),
            dma, dma, dma((3,)), dma((3,)), dma((3,)), dma((3,)),
        ],
        compiler_params=pltpu.CompilerParams(collective_id=0, has_side_effects=True),
        name="merge_and_gather",
    )(*w, *a, *b, *norms)


def local(w_gate, low_gate, high_gate, w_up, low_up, high_up, w_down, low_down, high_down, norm_train, norm_step):
    gate, up, down, norm = gathered(
        w_gate.T, w_up.T, w_down, high_gate, high_up, low_down.T, low_gate.T, low_up.T, high_down,
        norm_train.reshape(1, 16), norm_step.reshape(1, 16))
    return gate.T, up.T, down, norm.reshape(-1)


def solution(mesh):
    finer = Mesh(mesh.devices.reshape(8, 2, 4, 4), AXES)
    in_specs = (
        P(FSDP, TP), P(FSDP, None), P(None, TP),
        P(FSDP, TP), P(FSDP, None), P(None, TP),
        P(TP, FSDP), P(TP, None), P(None, FSDP),
        P(FSDP + TP), P(FSDP + TP),
    )
    out_specs = (P(None, TP), P(None, TP), P(TP, None), P())
    return jax.shard_map(local, mesh=finer, in_specs=in_specs, out_specs=out_specs, check_vma=False)
```

time: 140 us -> 109 us (0.78)
  Pallas kernels: 0 us -> 95.9 us
  waiting for transfers between devices: 57 us -> 0 us
  blocking collectives: 47.1 us -> 0 us
  between operations: 14.8 us -> 0.66 us
  matrix products: 3.94 us -> 0 us
  local copies, waits for them, and re-layouts: 15.8 us -> 12.7 us
    pallas_call x0 -> x1, Pallas kernels: none -> 95.9 us  [gathered(): pl.pallas_call(functools.partial(body, rows, width), out_shape=(whole, wh...]
    all_gather x1 -> x0, waiting for transfers between devices: 57 us -> none  [gather_turned(): whole = lax.all_gather(both, axis, axis=0, tiled=True)]
    all_gather x3 -> x0, blocking collectives: 29.8 us -> none  [all_blocks(): parts = lax.all_gather(parts, axes[k], axis=0, tiled=True)]
    unnamed x1 -> x0, blocking collectives: 17.3 us -> none
    transpose x2 -> x0, local copies, waits for them, and re-layouts: 13.3 us -> none  [the longest x1 13.3 us: gather_turned(): jnp.moveaxis(b.reshape(-1, *t.shape[1:]), 0, dim)]
    unnamed x12, local copies, waits for them, and re-layouts: 1.62 us -> 12.7 us
    dot_general x3 -> x0, matrix products: 3.94 us -> none  [the longest x1 1.32 us: local(): jnp.dot(low_down, high_down, preferred_element_type=jnp.float32)]
  transfers between devices with their start and end apart: 1 -> 0, of which waited for: 1 -> 0; matrix products, arithmetic and copies ran while one was open for 1% -> 0% of each run, Pallas kernels for 0% -> 0%
where the time goes in v1:
time: 109 us
  Pallas kernels  95.9 us (88%)
  local copies, waits for them, and re-layouts  12.7 us (12%)
    pallas_call x1, Pallas kernels, gathered(): pl.pallas_call(functools.partial(body, rows, width), out_shape=(whole, wh...  95.9 us
    unnamed x12, local copies, waits for them, and re-layouts  12.7 us

profile of v1, /device:TPU:1, one launch (start us, length us, event | category | flops | bytes accessed | tf_op | source)
XLA Modules:
  0.0 109.3 jit_solution(466445370662512158)
XLA Ops:
  0.6 95.9 %merge_and_gather.1 = (bf16[688,4096]{1,0:T(8,128)(2,1)}, bf16[688,4096]{1,0:T(8,128)(2,1)}, bf16[688,4096]{1,0:T(8,128)(2,1)}, bf16[32,128]{1,0:T(8,128)(2,1)}) custom-call(bf16[688,256]{1,0:T(8,128)(2,1)} %bitcast.14, bf16[688,256]{1,0:T(8,128)(2,1)} %bitcast.15, bf16[688,256]{1,0:T(8,128)(2,1)} %refs_2_.1, bf16[16,688]{1,0:T(8,128)(2,1)} %refs_3_.1, ...), custom_call_target="tpu_custom_call" | custom-call | tf_op jit(solution)/shard_map/merge_and_gather/pallas_call | solution.py:252
  96.6 0.0 copy-start
  96.6 0.0 slice-start
  96.6 6.3 %copy.19 = bf16[4096,688]{0,1:T(8,128)(2,1)} copy(bf16[4096,688]{0,1:T(8,128)(2,1)} %bitcast.13) | data formatting | bytes 11272192
  102.9 0.0 copy-done
  102.9 0.0 slice-start.1
  102.9 2.6 %copy.20 = bf16[4096,688]{0,1:T(8,128)(2,1)} copy(bf16[4096,688]{0,1:T(8,128)(2,1)S(1)} %bitcast.12) | data formatting | bytes 11272192
  105.5 0.0 slice-done
  105.5 0.7 slice-done.1
  106.2 0.0 copy-start.1
  106.2 2.5 %copy.21 = bf16[688,4096]{1,0:T(8,128)(2,1)} copy(bf16[688,4096]{1,0:T(8,128)(2,1)S(1)} %bitcast.11) | data formatting | bytes 11272192
  108.7 0.0 copy-done.1
  108.7 0.6 copy.22
  (1 shorter events, 0.0 us)
Async XLA Ops:
  96.6 6.3 %copy-start = (bf16[688,4096]{1,0:T(8,128)(2,1)S(1)}, bf16[688,4096]{1,0:T(8,128)(2,1)}, u32[]{:S(2)}) copy-start(bf16[688,4096]{1,0:T(8,128)(2,1)} %get-tuple-element.9) | copy-start | bytes 16908292
  96.6 8.9 %slice-start = ((s8[5636096]{0:T(1024)(128)(4,1)}), s8[4194304]{0:T(1024)(128)(4,1)S(1)}, s32[]{:S(2)}) async-start(s8[5636096]{0:T(1024)(128)(4,1)} %bitcast.10), calls=%async_computation | async-start | bytes 8388608
  102.9 3.3 %slice-start.1 = ((s8[5636096]{0:T(1024)(128)(4,1)}), s8[1441792]{0:T(1024)(128)(4,1)S(1)}, s32[]{:S(2)}) async-start(s8[5636096]{0:T(1024)(128)(4,1)} %bitcast.10), calls=%async_computation.1 | async-start | bytes 2883584
  106.2 2.5 %copy-start.1 = (bf16[32,128]{1,0:T(8,128)(2,1)S(1)}, bf16[32,128]{1,0:T(8,128)(2,1)}, u32[]{:S(2)}) copy-start(bf16[32,128]{1,0:T(8,128)(2,1)} %get-tuple-element.11) | copy-start | bytes 24580

commit v2 on v1

v2 whole, which is shorter than its diff:
```python
import functools

import jax
import jax.numpy as jnp
from jax import lax
from jax.experimental import pallas as pl
from jax.experimental.pallas import tpu as pltpu
from jax.sharding import Mesh
from jax.sharding import PartitionSpec as P

mix_rate = 2.0
SHIFT = 0
LEAD = 2
NORM_AT = 3
MESH = pl.DeviceIdType.MESH
AXES = ("z", "core", "y", "x")
FSDP = ("z", "core")
TP = ("y", "x")
NZ, NX, NY = 8, 4, 4
PIECES = (((0, 344), (344, 344), (688, 344), (1032, 344), (1376, 344), (1720, 344)),) * 4
MOST = max(len(p) for p in PIECES)


def body(rows, *refs):
    (wg, wu, wd, ag, au, ad, bg, bu, bd, ntrain, nstep, blocks, onorm,
     w_v, a_v, b_v, nt_v, ns_v, nz, ncore, nx, ny, nrow,
     in_sem, r_recv, l_recv, s_recv, r_send, l_send, s_send,
     nrr, nlr, nrs, nls, nsr, nss, nxr, nxs, nyr, nys,
     right_in, left_in, x_in, y_in, sib_in) = refs
    w_hbm, a_hbm, b_hbm = (wg, wu, wd), (ag, au, ad), (bg, bu, bd)
    z, core, y, x = (lax.axis_index(k) for k in AXES)
    right, left = {"z": lax.rem(z + 1, NZ)}, {"z": lax.rem(z + NZ - 1, NZ)}
    sib = {"core": 1 - core}

    barrier = pltpu.get_barrier_semaphore()

    def maybe(cond, act):
        @pl.when(cond)
        def _():
            act()

    def signal(sem, device):
        pl.semaphore_signal(sem, inc=1, device_id=device, device_id_type=MESH)

    def greet(at, last, up, down):
        @pl.when(at < last)
        def _():
            signal(barrier, up)

        @pl.when(at == 0)
        def _():
            signal(barrier, down)

    greet(z, NZ - 1, right, left)

    @pl.when(core == 1)
    def _():
        signal(barrier, sib)

    loads = []
    for m in range(3):
        loads.append([
            pltpu.make_async_copy(w_hbm[m], w_v.at[m], in_sem.at[m, 0]),
            pltpu.make_async_copy(a_hbm[m], a_v.at[m], in_sem.at[m, 1]),
            pltpu.make_async_copy(b_hbm[m], b_v.at[m], in_sem.at[m, 2]),
        ])
    norm_loads = [
        pltpu.make_async_copy(ntrain, nt_v, in_sem.at[3, 0]),
        pltpu.make_async_copy(nstep, ns_v, in_sem.at[3, 1]),
    ]
    for m in range(3):
        for copy in loads[m]:
            copy.start()
    for copy in norm_loads:
        copy.start()
    for k in range(1, NX):
        maybe(x + k < NX, lambda: signal(barrier, {"x": x + k}))
    for k in range(1, NY):
        maybe(y + k < NY, lambda: signal(barrier, {"y": y + k}))

    def greeted():
        def least(at, last):
            return jnp.where(at > 0, 1, 0) + jnp.where(at == last, 1, 0)

        greetings = least(z, NZ - 1) + x + y + (1 - core)
        maybe(greetings > 0, lambda: pl.semaphore_wait(barrier, greetings))

        @pl.when(z > 0)
        def _():
            signal(right_in, left)

        @pl.when(z == NZ - 1)
        def _():
            signal(left_in, right)

        @pl.when(core == 0)
        def _():
            signal(sib_in, sib)

        for k in range(1, NX):
            maybe(x - k >= 0, lambda: signal(x_in, {"x": x - k}))
        for k in range(1, NY):
            maybe(y - k >= 0, lambda: signal(y_in, {"y": y - k}))

    def spot(step, k, block_z, block_core):
        r0, n = PIECES[step][k]
        return blocks.at[block_z * 2 + block_core, pl.ds(r0, n), :]

    def remote(src, dst, send, recv, device):
        return pltpu.make_async_remote_copy(
            src_ref=src, dst_ref=dst, send_sem=send, recv_sem=recv, device_id=device, device_id_type=MESH)

    count = len(PIECES[3])

    def split(at):
        return count // 2 + jnp.where(at == NZ - 1, SHIFT, 0) - jnp.where(at == 0, SHIFT, 0)

    r_out, r_in = split(lax.rem(z + 1, NZ)), split(z)
    l_out, l_in = split(lax.rem(z + NZ - 1, NZ)), split(z)
    low, high = count // 2 - SHIFT, count // 2 + SHIFT

    def r_copy(step, k):
        at = spot(step, k, lax.rem(z + NZ - step, NZ), core)
        return remote(at, at, r_send.at[step, k], r_recv.at[step, k], right)

    def l_copy(step, k):
        at = spot(step, k, lax.rem(z + step, NZ), core)
        return remote(at, at, l_send.at[step, k], l_recv.at[step, k], left)

    def r_wait(step, k):
        at = spot(step, k, lax.rem(z + NZ - step - 1, NZ), core)
        remote(at, at, r_send.at[step, k], r_recv.at[step, k], right).wait_recv()

    def l_wait(step, k):
        at = spot(step, k, lax.rem(z + step + 1, NZ), core)
        remote(at, at, l_send.at[step, k], l_recv.at[step, k], left).wait_recv()

    def table(dist):
        return max(min(dist, NZ - dist) - 1, 0)

    def s_copy(dist, k):
        at = spot(table(dist), k, lax.rem(z + dist, NZ), core)
        return remote(at, at, s_send.at[dist, k], s_recv.at[dist, k], sib)

    def s_wait(dist, k):
        at = spot(table(dist), k, lax.rem(z + dist, NZ), 1 - core)
        remote(at, at, s_send.at[dist, k], s_recv.at[dist, k], sib).wait_recv()

    loaded = set()

    def compute(k):
        r0, n = PIECES[0][k]
        for m in range(3):
            at, end = max(r0, m * rows) - m * rows, min(r0 + n, (m + 1) * rows) - m * rows
            if at >= end:
                continue
            if m not in loaded:
                loaded.add(m)
                for copy in loads[m]:
                    copy.wait()
            delta = lax.dot_general(
                a_v[m, :, at:end], b_v[m], (((0,), (0,)), ((), ())), preferred_element_type=jnp.float32)
            whole = w_v[m, at:end, :].astype(jnp.float32) + mix_rate * delta
            blocks[z * 2 + core, m * rows + at:m * rows + end, :] = whole.astype(jnp.bfloat16)

    started = []

    def go(copy):
        copy.start()
        started.append(copy)

    def first_way(k):
        maybe(z > 0, lambda: l_copy(0, k).start())
        maybe(z == 0, lambda: r_copy(0, k).start())

    def second_way(k):
        maybe(z > 0, lambda: r_copy(0, k).start())
        maybe(z == 0, lambda: l_copy(0, k).start())

    def own_sent(k):
        started.append(r_copy(0, k))
        started.append(l_copy(0, k))

    def compute_all(at, end):
        for k in range(at, end):
            compute(k)
            if k == at:
                continue
            yield k - 1
        yield end - 1

    lead = LEAD
    for n, k in enumerate(compute_all(0, lead)):
        if n == 0:
            greeted()
            maybe(z == 0, lambda: pl.semaphore_wait(right_in, 1))
        first_way(k)
    maybe(jnp.logical_and(z > 0, z < NZ - 1), lambda: pl.semaphore_wait(right_in, 1))
    maybe(z == 0, lambda: pl.semaphore_wait(left_in, 1))
    for k in range(lead):
        second_way(k)
    def own_sib(k):
        own_sent(k)
        go(s_copy(0, k))

    for k in compute_all(lead, len(PIECES[0])):
        if k < NORM_AT:
            first_way(k)
            second_way(k)
    maybe(core == 1, lambda: pl.semaphore_wait(sib_in, 1))
    for k in range(NORM_AT):
        own_sib(k)

    for copy in norm_loads:
        copy.wait()
    gain = (nt_v[...] + ns_v[...]).astype(jnp.bfloat16)
    t = y * NX + x
    lane = lax.broadcasted_iota(jnp.int32, (16, 128), 1)
    entry = lax.broadcasted_iota(jnp.int32, (16, 128), 0)
    place = jnp.where(lane == lax.rem(t, 8) * 16 + entry, 1.0, 0.0).astype(jnp.bfloat16)
    spread = jnp.dot(jnp.broadcast_to(gain, (16, 16)), place, preferred_element_type=jnp.float32)[:8]
    row = lax.broadcasted_iota(jnp.int32, (8, 128), 0)
    nx[x] = jnp.where(row == core * 2 + t // 8, spread, 0.0)

    def spread_over(buf, at, size, axis, send, recv):
        copies = []
        for k in range(1, size):
            device = {axis: lax.rem(at + k, size)}
            copies.append(remote(buf.at[at], buf.at[at], send.at[k - 1], recv.at[k - 1], device))
            go(copies[-1])
        for k in range(1, size):
            source = lax.rem(at + size - k, size)
            remote(buf.at[source], buf.at[source], send.at[k - 1], recv.at[k - 1], {axis: source}).wait_recv()

    maybe(x < NX - 1, lambda: pl.semaphore_wait(x_in, NX - 1 - x))
    maybe(y < NY - 1, lambda: pl.semaphore_wait(y_in, NY - 1 - y))
    spread_over(nx, x, NX, "x", nxs, nxr)
    ny[y] = nx[0] + nx[1] + nx[2] + nx[3]
    spread_over(ny, y, NY, "y", nys, nyr)
    ncore[core] = ny[0] + ny[1] + ny[2] + ny[3]
    go(remote(ncore.at[core], ncore.at[core], nss, nsr, sib))
    remote(ncore.at[1 - core], ncore.at[1 - core], nss, nsr, sib).wait_recv()
    nz[z] = (ncore[0] + ncore[1]).astype(jnp.bfloat16)

    def norm_r(step):
        at = nz.at[lax.rem(z + NZ - step, NZ)]
        return remote(at, at, nrs.at[step], nrr.at[step], right)

    def norm_l(step):
        at = nz.at[lax.rem(z + step, NZ)]
        return remote(at, at, nls.at[step], nlr.at[step], left)

    def norm_step(step):
        at = nz.at[lax.rem(z + NZ - step - 1, NZ)]
        remote(at, at, nrs.at[step], nrr.at[step], right).wait_recv()
        if step < 3:
            go(norm_r(step + 1))
            at = nz.at[lax.rem(z + step + 1, NZ)]
            remote(at, at, nls.at[step], nlr.at[step], left).wait_recv()
            if step < 2:
                go(norm_l(step + 1))

    go(norm_r(0))
    go(norm_l(0))
    for k in range(NORM_AT, len(PIECES[0])):
        first_way(k)
        second_way(k)
        own_sib(k)

    parted = []

    def part(cond, copy):
        maybe(cond, copy.start)
        parted.append((cond, copy))

    def inside(piece, held):
        return all(any(r0 <= row < r0 + n for r0, n in held) for row in range(piece[0], piece[0] + piece[1], 4))

    for step in range(3):
        after = PIECES[step + 1]
        waiting = [list(range(len(after))), list(range(len(after)))]
        for k, piece in enumerate(PIECES[step]):
            if k == min(NORM_AT, len(PIECES[step]) - 1):
                norm_step(step)
            for way, (wait, copy, dist) in enumerate(((r_wait, r_copy, NZ - step - 1), (l_wait, l_copy, step + 1))):
                wait(step, k)
                while waiting[way] and inside(after[waiting[way][0]], PIECES[step][:k + 1]):
                    p = waiting[way].pop(0)
                    if step < 2:
                        go(copy(step + 1, p))
                    elif (p < low) if way == 0 else (p >= high):
                        go(copy(step + 1, p))
                    elif low <= p < high:
                        part(p < r_out if way == 0 else p >= l_out, copy(step + 1, p))
                go(s_copy(dist, k))

    for k in [v for pair in zip(range(count // 2), range(count // 2, count)) for v in pair]:
        if k < low:
            r_wait(3, k)
        elif k >= high:
            l_wait(3, k)
        else:
            maybe(k < r_in, lambda: r_wait(3, k))
            maybe(k >= l_in, lambda: l_wait(3, k))
        go(s_copy(4, k))

    norm_step(3)
    for k in range(NZ):
        nrow[4 * k:4 * k + 4, :] = nz[k, 0:4, :].astype(jnp.float32)
    onorm[...] = nrow[...].astype(jnp.bfloat16)

    for copy in started:
        copy.wait_send()
    for cond, copy in parted:
        maybe(cond, copy.wait_send)
    for dist in range(NZ):
        for k in range(len(PIECES[table(dist)])):
            s_wait(dist, k)


def gathered(*args):
    w, a, b, norms = args[0:3], args[3:6], args[6:9], args[9:11]
    rows, width = w[0].shape
    rank = a[0].shape[0]
    whole = pltpu.VMEM((16, 3 * rows, width), jnp.bfloat16)
    vmem = pl.BlockSpec(memory_space=pltpu.VMEM)
    hbm = pl.BlockSpec(memory_space=pltpu.HBM)
    dma = pltpu.SemaphoreType.DMA
    regular = pltpu.SemaphoreType.REGULAR
    f32 = jnp.float32
    return pl.pallas_call(
        functools.partial(body, rows),
        out_shape=(whole, pltpu.VMEM((32, 128), jnp.bfloat16)),
        in_specs=[hbm] * 11,
        out_specs=(vmem,) * 2,
        scratch_shapes=[
            pltpu.VMEM((3, rows, width), jnp.bfloat16),
            pltpu.VMEM((3, rank, rows), jnp.bfloat16),
            pltpu.VMEM((3, rank, width), jnp.bfloat16),
            pltpu.VMEM((1, 16), f32),
            pltpu.VMEM((1, 16), f32),
            pltpu.VMEM((8, 8, 128), jnp.bfloat16),
            pltpu.VMEM((2, 8, 128), f32),
            pltpu.VMEM((4, 8, 128), f32),
            pltpu.VMEM((4, 8, 128), f32),
            pltpu.VMEM((32, 128), f32),
            dma((4, 3)),
            dma((4, MOST)), dma((4, MOST)), dma((8, MOST)),
            dma((4, MOST)), dma((4, MOST)), dma((8, MOST)),
            dma((4,)), dma((4,)), dma((4,)), dma((4,)),
            dma, dma, dma((3,)), dma((3,)), dma((3,)), dma((3,)),
            regular, regular, regular, regular, regular,
        ],
        compiler_params=pltpu.CompilerParams(collective_id=0, has_side_effects=True, vmem_limit_bytes=30 * 2**20),
        name="merge_and_gather",
    )(*[pltpu.with_memory_space_constraint(v, pltpu.HBM) for v in (*w, *a, *b, *norms)])


def write_out(blocks, row, gate, up, down, norm, sems):
    rows, width = gate.shape[0], blocks.shape[2]
    copies = [pltpu.make_async_copy(row, norm, sems.at[3, 0])]
    for m, out in enumerate((gate, up, down)):
        for f in range(blocks.shape[0]):
            copies.append(pltpu.make_async_copy(
                blocks.at[f, pl.ds(m * rows, rows), :], out.at[:, pl.ds(f * width, width)], sems.at[m, f]))
    for copy in copies:
        copy.start()
    for copy in copies:
        copy.wait()


def written(blocks, row):
    count, rows, width = blocks.shape
    whole = jax.ShapeDtypeStruct((rows // 3, count * width), blocks.dtype)
    return pl.pallas_call(
        write_out,
        out_shape=(whole, whole, whole, jax.ShapeDtypeStruct(row.shape, row.dtype)),
        in_specs=[pl.BlockSpec(memory_space=pltpu.VMEM)] * 2,
        out_specs=(pl.BlockSpec(memory_space=pltpu.HBM),) * 4,
        scratch_shapes=[pltpu.SemaphoreType.DMA((4, count))],
        compiler_params=pltpu.CompilerParams(vmem_limit_bytes=2**20),
        name="write_out",
    )(blocks, row)


def local(w_gate, low_gate, high_gate, w_up, low_up, high_up, w_down, low_down, high_down, norm_train, norm_step):
    blocks, row = gathered(
        w_gate.T, w_up.T, w_down, high_gate, high_up, low_down.T, low_gate.T, low_up.T, high_down,
        norm_train.reshape(1, 16), norm_step.reshape(1, 16))
    gate, up, down, norm = written(blocks, row)
    return gate.T, up.T, down, norm.reshape(-1)


def solution(mesh):
    finer = Mesh(mesh.devices.reshape(8, 2, 4, 4), AXES)
    in_specs = (
        P(FSDP, TP), P(FSDP, None), P(None, TP),
        P(FSDP, TP), P(FSDP, None), P(None, TP),
        P(TP, FSDP), P(TP, None), P(None, FSDP),
        P(FSDP + TP), P(FSDP + TP),
    )
    out_specs = (P(None, TP), P(None, TP), P(TP, None), P())
    return jax.shard_map(local, mesh=finer, in_specs=in_specs, out_specs=out_specs, check_vma=False)
```

time: 109 us -> 99.3 us (0.911)
  local copies, waits for them, and re-layouts: 12.7 us -> 0 us
  Pallas kernels: 95.9 us -> 98.6 us
    unnamed x12 -> x0, local copies, waits for them, and re-layouts: 12.7 us -> none
    pallas_call x1 -> x2, Pallas kernels: 95.9 us -> 98.6 us  [the longest x1 92.2 us: gathered(): pl.pallas_call(functools.partial(body, rows), out_shape=(whole, pltpu.VME...]
where the time goes in v2:
time: 99.3 us; the launch traced here: 99.2 us
  Pallas kernels  98.6 us (99%)
    pallas_call x1, Pallas kernels, gathered(): pl.pallas_call(functools.partial(body, rows), out_shape=(whole, pltpu.VME...  92.2 us
    pallas_call x1, Pallas kernels, written(): pl.pallas_call(write_out, out_shape=(whole, whole, whole, jax.ShapeDtypeS...  6.4 us

profile of v2, /device:TPU:1, one launch (start us, length us, event | category | flops | bytes accessed | tf_op | source)
XLA Modules:
  0.0 99.2 jit_solution(11204540813927384006)
XLA Ops:
  0.6 92.2 %merge_and_gather.1 = (bf16[16,2064,256]{2,1,0:T(8,128)(2,1)S(1)}, bf16[32,128]{1,0:T(8,128)(2,1)S(1)}) custom-call(bf16[688,256]{1,0:T(8,128)(2,1)} %bitcast.10, bf16[688,256]{1,0:T(8,128)(2,1)} %bitcast.11, bf16[688,256]{1,0:T(8,128)(2,1)} %refs_2_.1, bf16[16,688]{1,0:T(8,128)(2,1)} %refs_3_.1, bf16[16,688]{1,0:T(8,128)(2,1)} %refs_4_.1, ...), custom_call_target="tpu_custom_call" | custom-call | tf_op jit(solution)/shard_map/merge_and_gather/pallas_call | solution.py:331
  92.8 6.4 %write_out.1 = (bf16[688,4096]{1,0:T(8,128)(2,1)}, bf16[688,4096]{1,0:T(8,128)(2,1)}, bf16[688,4096]{1,0:T(8,128)(2,1)}, bf16[32,128]{1,0:T(8,128)(2,1)}) custom-call(bf16[16,2064,256]{2,1,0:T(8,128)(2,1)S(1)} %get-tuple-element.10.blocks, bf16[32,128]{1,0:T(8,128)(2,1)S(1)} %get-tuple-element.11.row), custom_call_target="tpu_custom_call" | custom-call | tf_op jit(solution)/shard_map/write_out/pallas_call | solution.py:375

commit v3 on v2

--- a/solution.py
+++ b/solution.py
@@ -9,15 +9,14 @@
 from jax.sharding import PartitionSpec as P
 
 mix_rate = 2.0
-SHIFT = 0
+SHIFT = 1
 LEAD = 2
-NORM_AT = 3
 MESH = pl.DeviceIdType.MESH
 AXES = ("z", "core", "y", "x")
 FSDP = ("z", "core")
 TP = ("y", "x")
 NZ, NX, NY = 8, 4, 4
-PIECES = (((0, 344), (344, 344), (688, 344), (1032, 344), (1376, 344), (1720, 344)),) * 4
+PIECES = (((0, 88), (88, 432), (520, 512), (1032, 520), (1552, 512)), ((0, 520), (520, 512), (1032, 520), (1552, 512)), ((0, 520), (520, 512), (1032, 520), (1552, 512)), ((0, 520), (520, 256), (776, 256), (1032, 256), (1288, 256), (1544, 520)))
 MOST = max(len(p) for p in PIECES)
 
 
@@ -25,8 +24,8 @@
     (wg, wu, wd, ag, au, ad, bg, bu, bd, ntrain, nstep, blocks, onorm,
      w_v, a_v, b_v, nt_v, ns_v, nz, ncore, nx, ny, nrow,
      in_sem, r_recv, l_recv, s_recv, r_send, l_send, s_send,
-     nrr, nlr, nrs, nls, nsr, nss, nxr, nxs, nyr, nys,
-     right_in, left_in, x_in, y_in, sib_in) = refs
+     nzr, nzs, nsr, nss, nxr, nxs, nyr, nys,
+     right_in, left_in, z_in, x_in, y_in, sib_in) = refs
     w_hbm, a_hbm, b_hbm = (wg, wu, wd), (ag, au, ad), (bg, bu, bd)
     z, core, y, x = (lax.axis_index(k) for k in AXES)
     right, left = {"z": lax.rem(z + 1, NZ)}, {"z": lax.rem(z + NZ - 1, NZ)}
@@ -42,16 +41,8 @@
     def signal(sem, device):
         pl.semaphore_signal(sem, inc=1, device_id=device, device_id_type=MESH)
 
-    def greet(at, last, up, down):
-        @pl.when(at < last)
-        def _():
-            signal(barrier, up)
-
-        @pl.when(at == 0)
-        def _():
-            signal(barrier, down)
-
-    greet(z, NZ - 1, right, left)
+    for k in range(1, NZ):
+        maybe(z + k < NZ, lambda: signal(barrier, {"z": z + k}))
 
     @pl.when(core == 1)
     def _():
@@ -79,10 +70,7 @@
         maybe(y + k < NY, lambda: signal(barrier, {"y": y + k}))
 
     def greeted():
-        def least(at, last):
-            return jnp.where(at > 0, 1, 0) + jnp.where(at == last, 1, 0)
-
-        greetings = least(z, NZ - 1) + x + y + (1 - core)
+        greetings = x + y + z + (1 - core)
         maybe(greetings > 0, lambda: pl.semaphore_wait(barrier, greetings))
 
         @pl.when(z > 0)
@@ -97,6 +85,8 @@
         def _():
             signal(sib_in, sib)
 
+        for k in range(1, NZ):
+            maybe(z - k >= 0, lambda: signal(z_in, {"z": z - k}))
         for k in range(1, NX):
             maybe(x - k >= 0, lambda: signal(x_in, {"x": x - k}))
         for k in range(1, NY):
@@ -190,25 +180,25 @@
         yield end - 1
 
     lead = LEAD
+    greeted()
     for n, k in enumerate(compute_all(0, lead)):
         if n == 0:
-            greeted()
             maybe(z == 0, lambda: pl.semaphore_wait(right_in, 1))
         first_way(k)
     maybe(jnp.logical_and(z > 0, z < NZ - 1), lambda: pl.semaphore_wait(right_in, 1))
     maybe(z == 0, lambda: pl.semaphore_wait(left_in, 1))
     for k in range(lead):
         second_way(k)
+
     def own_sib(k):
         own_sent(k)
         go(s_copy(0, k))
 
     for k in compute_all(lead, len(PIECES[0])):
-        if k < NORM_AT:
-            first_way(k)
-            second_way(k)
+        first_way(k)
+        second_way(k)
     maybe(core == 1, lambda: pl.semaphore_wait(sib_in, 1))
-    for k in range(NORM_AT):
+    for k in range(len(PIECES[0])):
         own_sib(k)
 
     for copy in norm_loads:
@@ -223,11 +213,11 @@
     nx[x] = jnp.where(row == core * 2 + t // 8, spread, 0.0)
 
     def spread_over(buf, at, size, axis, send, recv):
-        copies = []
         for k in range(1, size):
             device = {axis: lax.rem(at + k, size)}
-            copies.append(remote(buf.at[at], buf.at[at], send.at[k - 1], recv.at[k - 1], device))
-            go(copies[-1])
+            go(remote(buf.at[at], buf.at[at], send.at[k - 1], recv.at[k - 1], device))
+
+    def collect(buf, at, size, axis, send, recv):
         for k in range(1, size):
             source = lax.rem(at + size - k, size)
             remote(buf.at[source], buf.at[source], send.at[k - 1], recv.at[k - 1], {axis: source}).wait_recv()
@@ -235,37 +225,17 @@
     maybe(x < NX - 1, lambda: pl.semaphore_wait(x_in, NX - 1 - x))
     maybe(y < NY - 1, lambda: pl.semaphore_wait(y_in, NY - 1 - y))
     spread_over(nx, x, NX, "x", nxs, nxr)
+    collect(nx, x, NX, "x", nxs, nxr)
     ny[y] = nx[0] + nx[1] + nx[2] + nx[3]
     spread_over(ny, y, NY, "y", nys, nyr)
+    collect(ny, y, NY, "y", nys, nyr)
     ncore[core] = ny[0] + ny[1] + ny[2] + ny[3]
     go(remote(ncore.at[core], ncore.at[core], nss, nsr, sib))
     remote(ncore.at[1 - core], ncore.at[1 - core], nss, nsr, sib).wait_recv()
-    nz[z] = (ncore[0] + ncore[1]).astype(jnp.bfloat16)
-
-    def norm_r(step):
-        at = nz.at[lax.rem(z + NZ - step, NZ)]
-        return remote(at, at, nrs.at[step], nrr.at[step], right)
-
-    def norm_l(step):
-        at = nz.at[lax.rem(z + step, NZ)]
-        return remote(at, at, nls.at[step], nlr.at[step], left)
-
-    def norm_step(step):
-        at = nz.at[lax.rem(z + NZ - step - 1, NZ)]
-        remote(at, at, nrs.at[step], nrr.at[step], right).wait_recv()
-        if step < 3:
-            go(norm_r(step + 1))
-            at = nz.at[lax.rem(z + step + 1, NZ)]
-            remote(at, at, nls.at[step], nlr.at[step], left).wait_recv()
-            if step < 2:
-                go(norm_l(step + 1))
-
-    go(norm_r(0))
-    go(norm_l(0))
-    for k in range(NORM_AT, len(PIECES[0])):
-        first_way(k)
-        second_way(k)
-        own_sib(k)
+    nz[z] = (ncore[0] + ncore[1])[0:4].astype(jnp.bfloat16)
+
+    maybe(z < NZ - 1, lambda: pl.semaphore_wait(z_in, NZ - 1 - z))
+    spread_over(nz, z, NZ, "z", nzs, nzr)
 
     parted = []
 
@@ -279,9 +249,9 @@
     for step in range(3):
         after = PIECES[step + 1]
         waiting = [list(range(len(after))), list(range(len(after)))]
+        if step == 2:
+            waiting = [list(range(high)), [*range(high, count), *reversed(range(low, high))]]
         for k, piece in enumerate(PIECES[step]):
-            if k == min(NORM_AT, len(PIECES[step]) - 1):
-                norm_step(step)
             for way, (wait, copy, dist) in enumerate(((r_wait, r_copy, NZ - step - 1), (l_wait, l_copy, step + 1))):
                 wait(step, k)
                 while waiting[way] and inside(after[waiting[way][0]], PIECES[step][:k + 1]):
@@ -294,7 +264,7 @@
                         part(p < r_out if way == 0 else p >= l_out, copy(step + 1, p))
                 go(s_copy(dist, k))
 
-    for k in [v for pair in zip(range(count // 2), range(count // 2, count)) for v in pair]:
+    for k in [v for pair in zip(range(low), range(high, count)) for v in pair] + list(range(low, high)):
         if k < low:
             r_wait(3, k)
         elif k >= high:
@@ -304,9 +274,9 @@
             maybe(k >= l_in, lambda: l_wait(3, k))
         go(s_copy(4, k))
 
-    norm_step(3)
+    collect(nz, z, NZ, "z", nzs, nzr)
     for k in range(NZ):
-        nrow[4 * k:4 * k + 4, :] = nz[k, 0:4, :].astype(jnp.float32)
+        nrow[4 * k:4 * k + 4, :] = nz[k].astype(jnp.float32)
     onorm[...] = nrow[...].astype(jnp.bfloat16)
 
     for copy in started:
@@ -339,7 +309,7 @@
             pltpu.VMEM((3, rank, width), jnp.bfloat16),
             pltpu.VMEM((1, 16), f32),
             pltpu.VMEM((1, 16), f32),
-            pltpu.VMEM((8, 8, 128), jnp.bfloat16),
+            pltpu.VMEM((8, 4, 128), jnp.bfloat16),
             pltpu.VMEM((2, 8, 128), f32),
             pltpu.VMEM((4, 8, 128), f32),
             pltpu.VMEM((4, 8, 128), f32),
@@ -347,9 +317,8 @@
             dma((4, 3)),
             dma((4, MOST)), dma((4, MOST)), dma((8, MOST)),
             dma((4, MOST)), dma((4, MOST)), dma((8, MOST)),
-            dma((4,)), dma((4,)), dma((4,)), dma((4,)),
-            dma, dma, dma((3,)), dma((3,)), dma((3,)), dma((3,)),
-            regular, regular, regular, regular, regular,
+            dma((7,)), dma((7,)), dma, dma, dma((3,)), dma((3,)), dma((3,)), dma((3,)),
+            regular, regular, regular, regular, regular, regular,
         ],
         compiler_params=pltpu.CompilerParams(collective_id=0, has_side_effects=True, vmem_limit_bytes=30 * 2**20),
         name="merge_and_gather",
@@ -359,8 +328,8 @@
 def write_out(blocks, row, gate, up, down, norm, sems):
     rows, width = gate.shape[0], blocks.shape[2]
     copies = [pltpu.make_async_copy(row, norm, sems.at[3, 0])]
-    for m, out in enumerate((gate, up, down)):
-        for f in range(blocks.shape[0]):
+    for f in range(blocks.shape[0]):
+        for m, out in enumerate((gate, up, down)):
             copies.append(pltpu.make_async_copy(
                 blocks.at[f, pl.ds(m * rows, rows), :], out.at[:, pl.ds(f * width, width)], sems.at[m, f]))
     for copy in copies:

time: 99.3 us -> 98.2 us (0.989)
  Pallas kernels: 98.6 us -> 97.5 us
    pallas_call x1, Pallas kernels: 92.2 us -> 91.1 us  [gathered(): pl.pallas_call(functools.partial(body, rows), out_shape=(whole, pltpu.VME...]
where the time goes in v3:
time: 98.2 us; the launch traced here: 98.1 us
  Pallas kernels  97.5 us (99%)
    pallas_call x1, Pallas kernels, gathered(): pl.pallas_call(functools.partial(body, rows), out_shape=(whole, pltpu.VME...  91.1 us
    pallas_call x1, Pallas kernels, written(): pl.pallas_call(write_out, out_shape=(whole, whole, whole, jax.ShapeDtypeS...  6.4 us

profile of v3, /device:TPU:1, one launch (start us, length us, event | category | flops | bytes accessed | tf_op | source)
XLA Modules:
  0.0 98.1 jit_solution(14969841000327175956)
XLA Ops:
  0.6 91.1 %merge_and_gather.1 = (bf16[16,2064,256]{2,1,0:T(8,128)(2,1)S(1)}, bf16[32,128]{1,0:T(8,128)(2,1)S(1)}) custom-call(bf16[688,256]{1,0:T(8,128)(2,1)} %bitcast.10, bf16[688,256]{1,0:T(8,128)(2,1)} %bitcast.11, bf16[688,256]{1,0:T(8,128)(2,1)} %refs_2_.1, bf16[16,688]{1,0:T(8,128)(2,1)} %refs_3_.1, bf16[16,688]{1,0:T(8,128)(2,1)} %refs_4_.1, ...), custom_call_target="tpu_custom_call" | custom-call | tf_op jit(solution)/shard_map/merge_and_gather/pallas_call | solution.py:301
  91.7 6.4 %write_out.1 = (bf16[688,4096]{1,0:T(8,128)(2,1)}, bf16[688,4096]{1,0:T(8,128)(2,1)}, bf16[688,4096]{1,0:T(8,128)(2,1)}, bf16[32,128]{1,0:T(8,128)(2,1)}) custom-call(bf16[16,2064,256]{2,1,0:T(8,128)(2,1)S(1)} %get-tuple-element.10.blocks, bf16[32,128]{1,0:T(8,128)(2,1)S(1)} %get-tuple-element.11.row), custom_call_target="tpu_custom_call" | custom-call | tf_op jit(solution)/shard_map/write_out/pallas_call | solution.py:344

commit v4 on v3

--- a/solution.py
+++ b/solution.py
@@ -16,8 +16,19 @@
 FSDP = ("z", "core")
 TP = ("y", "x")
 NZ, NX, NY = 8, 4, 4
-PIECES = (((0, 88), (88, 432), (520, 512), (1032, 520), (1552, 512)), ((0, 520), (520, 512), (1032, 520), (1552, 512)), ((0, 520), (520, 512), (1032, 520), (1552, 512)), ((0, 520), (520, 256), (776, 256), (1032, 256), (1288, 256), (1544, 520)))
-MOST = max(len(p) for p in PIECES)
+PIECES = (((0, 88), (88, 432), (520, 512), (1032, 520), (1552, 512)), ((0, 520), (520, 512), (1032, 520), (1552, 512)), ((0, 520), (520, 512), (1032, 520), (1552, 512)), ((0, 520), (520, 280), (800, 232), (1032, 200), (1232, 312), (1544, 520)))
+
+
+def flat(step, k):
+    return sum(len(p) for p in PIECES[:step]) + k
+
+
+def table(dist):
+    return max(min(dist, NZ - dist) - 1, 0)
+
+
+def flat_sib(dist, k):
+    return sum(len(PIECES[table(d)]) for d in range(dist)) + k
 
 
 def body(rows, *refs):
@@ -111,30 +122,27 @@
 
     def r_copy(step, k):
         at = spot(step, k, lax.rem(z + NZ - step, NZ), core)
-        return remote(at, at, r_send.at[step, k], r_recv.at[step, k], right)
+        return remote(at, at, r_send.at[1 + k if step == 3 else 0], r_recv.at[flat(step, k)], right)
 
     def l_copy(step, k):
         at = spot(step, k, lax.rem(z + step, NZ), core)
-        return remote(at, at, l_send.at[step, k], l_recv.at[step, k], left)
+        return remote(at, at, l_send.at[1 + k if step == 3 else 0], l_recv.at[flat(step, k)], left)
 
     def r_wait(step, k):
         at = spot(step, k, lax.rem(z + NZ - step - 1, NZ), core)
-        remote(at, at, r_send.at[step, k], r_recv.at[step, k], right).wait_recv()
+        remote(at, at, r_send.at[0], r_recv.at[flat(step, k)], right).wait_recv()
 
     def l_wait(step, k):
         at = spot(step, k, lax.rem(z + step + 1, NZ), core)
-        remote(at, at, l_send.at[step, k], l_recv.at[step, k], left).wait_recv()
-
-    def table(dist):
-        return max(min(dist, NZ - dist) - 1, 0)
+        remote(at, at, l_send.at[0], l_recv.at[flat(step, k)], left).wait_recv()
 
     def s_copy(dist, k):
         at = spot(table(dist), k, lax.rem(z + dist, NZ), core)
-        return remote(at, at, s_send.at[dist, k], s_recv.at[dist, k], sib)
+        return remote(at, at, s_send.at[0], s_recv.at[flat_sib(dist, k)], sib)
 
     def s_wait(dist, k):
         at = spot(table(dist), k, lax.rem(z + dist, NZ), 1 - core)
-        remote(at, at, s_send.at[dist, k], s_recv.at[dist, k], sib).wait_recv()
+        remote(at, at, s_send.at[0], s_recv.at[flat_sib(dist, k)], sib).wait_recv()
 
     loaded = set()
 
@@ -167,10 +175,6 @@
         maybe(z > 0, lambda: r_copy(0, k).start())
         maybe(z == 0, lambda: l_copy(0, k).start())
 
-    def own_sent(k):
-        started.append(r_copy(0, k))
-        started.append(l_copy(0, k))
-
     def compute_all(at, end):
         for k in range(at, end):
             compute(k)
@@ -191,8 +195,7 @@
         second_way(k)
 
     def own_sib(k):
-        own_sent(k)
-        go(s_copy(0, k))
+        s_copy(0, k).start()
 
     for k in compute_all(lead, len(PIECES[0])):
         first_way(k)
@@ -257,12 +260,12 @@
                 while waiting[way] and inside(after[waiting[way][0]], PIECES[step][:k + 1]):
                     p = waiting[way].pop(0)
                     if step < 2:
-                        go(copy(step + 1, p))
+                        copy(step + 1, p).start()
                     elif (p < low) if way == 0 else (p >= high):
                         go(copy(step + 1, p))
                     elif low <= p < high:
                         part(p < r_out if way == 0 else p >= l_out, copy(step + 1, p))
-                go(s_copy(dist, k))
+                s_copy(dist, k).start()
 
     for k in [v for pair in zip(range(low), range(high, count)) for v in pair] + list(range(low, high)):
         if k < low:
@@ -272,13 +275,16 @@
         else:
             maybe(k < r_in, lambda: r_wait(3, k))
             maybe(k >= l_in, lambda: l_wait(3, k))
-        go(s_copy(4, k))
+        s_copy(4, k).start()
 
     collect(nz, z, NZ, "z", nzs, nzr)
     for k in range(NZ):
         nrow[4 * k:4 * k + 4, :] = nz[k].astype(jnp.float32)
     onorm[...] = nrow[...].astype(jnp.bfloat16)
 
+    for count, sem in ((3, r_send), (3, l_send), (NZ, s_send)):
+        sent = blocks.at[pl.ds(0, count)]
+        remote(sent, sent, sem.at[0], r_recv.at[0], right).wait_send()
     for copy in started:
         copy.wait_send()
     for cond, copy in parted:
@@ -315,8 +321,8 @@
             pltpu.VMEM((4, 8, 128), f32),
             pltpu.VMEM((32, 128), f32),
             dma((4, 3)),
-            dma((4, MOST)), dma((4, MOST)), dma((8, MOST)),
-            dma((4, MOST)), dma((4, MOST)), dma((8, MOST)),
+            dma((flat(4, 0),)), dma((flat(4, 0),)), dma((flat_sib(NZ, 0),)),
+            dma((1 + len(PIECES[3]),)), dma((1 + len(PIECES[3]),)), dma((1,)),
             dma((7,)), dma((7,)), dma, dma, dma((3,)), dma((3,)), dma((3,)), dma((3,)),
             regular, regular, regular, regular, regular, regular,
         ],
@@ -327,15 +333,14 @@
 
 def write_out(blocks, row, gate, up, down, norm, sems):
     rows, width = gate.shape[0], blocks.shape[2]
-    copies = [pltpu.make_async_copy(row, norm, sems.at[3, 0])]
+    norm_copy = pltpu.make_async_copy(row, norm, sems.at[1])
+    norm_copy.start()
     for f in range(blocks.shape[0]):
         for m, out in enumerate((gate, up, down)):
-            copies.append(pltpu.make_async_copy(
-                blocks.at[f, pl.ds(m * rows, rows), :], out.at[:, pl.ds(f * width, width)], sems.at[m, f]))
-    for copy in copies:
-        copy.start()
-    for copy in copies:
-        copy.wait()
+            pltpu.make_async_copy(
+                blocks.at[f, pl.ds(m * rows, rows), :], out.at[:, pl.ds(f * width, width)], sems.at[0]).start()
+    norm_copy.wait()
+    pltpu.make_async_copy(blocks, blocks, sems.at[0]).wait()
 
 
 def written(blocks, row):
@@ -346,7 +351,7 @@
         out_shape=(whole, whole, whole, jax.ShapeDtypeStruct(row.shape, row.dtype)),
         in_specs=[pl.BlockSpec(memory_space=pltpu.VMEM)] * 2,
         out_specs=(pl.BlockSpec(memory_space=pltpu.HBM),) * 4,
-        scratch_shapes=[pltpu.SemaphoreType.DMA((4, count))],
+        scratch_shapes=[pltpu.SemaphoreType.DMA((2,))],
         compiler_params=pltpu.CompilerParams(vmem_limit_bytes=2**20),
         name="write_out",
     )(blocks, row)

time: 98.2 us -> 96.5 us (0.983)
  Pallas kernels: 97.5 us -> 95.8 us
    pallas_call x1, Pallas kernels: 91.1 us -> 89.9 us  [gathered(): pl.pallas_call(functools.partial(body, rows), out_shape=(whole, pltpu.VME...]
where the time goes in v4:
time: 96.5 us; the launch traced here: 96.4 us
  Pallas kernels  95.8 us (99%)
    pallas_call x1, Pallas kernels, gathered(): pl.pallas_call(functools.partial(body, rows), out_shape=(whole, pltpu.VME...  89.9 us
    pallas_call x1, Pallas kernels, written(): pl.pallas_call(write_out, out_shape=(whole, whole, whole, jax.ShapeDtypeS...  5.85 us

profile of v4, /device:TPU:1, one launch (start us, length us, event | category | flops | bytes accessed | tf_op | source)
XLA Modules:
  0.0 96.4 jit_solution(17594446906070709382)
XLA Ops:
  0.6 89.9 %merge_and_gather.1 = (bf16[16,2064,256]{2,1,0:T(8,128)(2,1)S(1)}, bf16[32,128]{1,0:T(8,128)(2,1)S(1)}) custom-call(bf16[688,256]{1,0:T(8,128)(2,1)} %bitcast.10, bf16[688,256]{1,0:T(8,128)(2,1)} %bitcast.11, bf16[688,256]{1,0:T(8,128)(2,1)} %refs_2_.1, bf16[16,688]{1,0:T(8,128)(2,1)} %refs_3_.1, bf16[16,688]{1,0:T(8,128)(2,1)} %refs_4_.1, ...), custom_call_target="tpu_custom_call" | custom-call | tf_op jit(solution)/shard_map/merge_and_gather/pallas_call | solution.py:307
  90.6 5.8 %write_out.1 = (bf16[688,4096]{1,0:T(8,128)(2,1)}, bf16[688,4096]{1,0:T(8,128)(2,1)}, bf16[688,4096]{1,0:T(8,128)(2,1)}, bf16[32,128]{1,0:T(8,128)(2,1)}) custom-call(bf16[16,2064,256]{2,1,0:T(8,128)(2,1)S(1)} %get-tuple-element.10.blocks, bf16[32,128]{1,0:T(8,128)(2,1)S(1)} %get-tuple-element.11.row), custom_call_target="tpu_custom_call" | custom-call | tf_op jit(solution)/shard_map/write_out/pallas_call | solution.py:349
